TPU v7x, 256 devices: a whole 4x4x8 slice. The times are simulated.
256 devices in a mesh: row: 32 (over x, y, z_lo), col: 8 (over z_hi, core).
Axes of the slice: x: 4, y: 4, z: 8 (z_hi: 4, z_lo: 2; z = z_hi * 2 + z_lo), core: 2. Of those that a mesh axis runs over, the one named last changes fastest.
Arguments:
- incident: bfloat16 [2, 65536, 512], P(None, ('row', 'col')), may hold values from -6 to 6
- near_tiles: bfloat16 [256, 2, 3, 2, 256, 256], P(('row', 'col')), may hold values from -0.15625 to 0.15625
- near_offsets: int32 [256, 3], P(('row', 'col')), may hold values from -2 to 2, as said below
- far_row: int32 [32, 8, 64], P('row', 'col'), may hold values from 0 to 7, as said below
- far_col: int32 [32, 8, 64], P('row', 'col'), may hold values from 0 to 31
- far_rank: int32 [32, 8, 64], P('row', 'col'), may hold values from 8 to 32, as said below
- far_count: int32 [32, 8], P('row', 'col'), may hold values from 8 to 64, as said below
- far_u: bfloat16 [32, 8, 2, 64, 2, 32, 256], P('row', 'col'), may hold values from -0.125 to 0.125
- far_v: bfloat16 [32, 8, 2, 64, 2, 32, 256], P('row', 'col'), may hold values from -0.25 to 0.25
Outputs:
- response: bfloat16 [2, 65536, 512], P(None, ('row', 'col'))
Inputs may be any that keep to these rules, and one draw needn't show every extreme that they name: `near_offsets`: slot 0 of every tile is 0; the other slots of a tile hold distinct values among -2, -1, 1, 2. On one device the pairs (far_row, far_col) of all 64 slots are distinct, and every block (i, j) they name has circular tile distance 3 or more between i and j. `far_rank`: slot 0 of every device has rank 32. `far_count`: some device has all 64 slots live.
All inputs are finite; a program needn't handle non-finite values.
Results may differ from a plain program's by a relative error of at most 0.0035.
Values may be sent and summed in bfloat16 or wider, within the bound.
A program may use at most 192 MiB of HBM per device.

v0:
```python
import jax
import jax.numpy as jnp
from jax import lax
from jax.sharding import PartitionSpec as P


def from_behind(value, axis, steps):
    count = lax.axis_size(axis)
    pairs = [(source, (source + steps) % count) for source in range(count)]
    return lax.ppermute(value, axis, pairs)


def combine_parts(real_prod, imag_prod):
    half_width = real_prod.shape[-1] // 2
    return jnp.concatenate(
        [
            real_prod[..., :half_width] - imag_prod[..., half_width:],
            real_prod[..., half_width:] + imag_prod[..., :half_width],
        ],
        axis=-1,
    )


def far_partial(
    wave_tiles,
    rows_local,
    cols_local,
    rank_local,
    live_count,
    u_wave,
    v_wave,
    group_limit,
    row_blocks,
):
    group_size = 16
    tile_rows = wave_tiles.shape[1]
    columns = wave_tiles.shape[2]
    rank_size = v_wave.shape[2]
    slot_ids = jnp.arange(group_size, dtype=jnp.int32)
    rank_ids = jnp.arange(rank_size, dtype=jnp.int32)

    def add_group(group_step, far_sum):
        first_slot = group_step * group_size
        rows_group = lax.dynamic_slice_in_dim(rows_local, first_slot, group_size)
        cols_group = lax.dynamic_slice_in_dim(cols_local, first_slot, group_size)
        rank_group = lax.dynamic_slice_in_dim(rank_local, first_slot, group_size)
        v_group = lax.dynamic_slice_in_dim(v_wave, first_slot, group_size, 0)
        u_group = lax.dynamic_slice_in_dim(u_wave, first_slot, group_size, 0)
        slot_tiles = jnp.take(wave_tiles, cols_group, axis=0)
        real_prod = jnp.einsum(
            "fkq,fqc->fkc", v_group[:, 0], slot_tiles, preferred_element_type=jnp.float32
        )
        imag_prod = jnp.einsum(
            "fkq,fqc->fkc", v_group[:, 1], slot_tiles, preferred_element_type=jnp.float32
        )
        live_mask = (first_slot + slot_ids < live_count)[:, None] & (
            rank_ids[None, :] < rank_group[:, None]
        )
        coefficients = (
            combine_parts(real_prod, imag_prod) * live_mask[:, :, None].astype(jnp.float32)
        ).astype(jnp.bfloat16)
        real_back = jnp.einsum(
            "fkp,fkc->fpc", u_group[:, 0], coefficients, preferred_element_type=jnp.float32
        )
        imag_back = jnp.einsum(
            "fkp,fkc->fpc", u_group[:, 1], coefficients, preferred_element_type=jnp.float32
        )
        contrib = combine_parts(real_back, imag_back)
        return far_sum.at[rows_group].add(contrib)

    zero_sum = jnp.zeros((row_blocks, tile_rows, columns), jnp.float32)
    return lax.fori_loop(0, group_limit, add_group, zero_sum)


def reduce_rows(far_sum, row_blocks, tile_rows, columns):
    flat_rows = far_sum.reshape(row_blocks * tile_rows, columns)
    return lax.psum_scatter(flat_rows, "col", scatter_dimension=0, tiled=True)


def shards(incident, near_tiles, near_offsets, far_row, far_col, far_rank, far_count, far_u, far_v):
    wave_count, tile_rows, columns = incident.shape
    row_blocks = lax.axis_size("col")
    stacked = []
    for shift_by in (2, 1, 0, -1, -2):
        if shift_by == 0:
            stacked.append(incident)
        else:
            stacked.append(from_behind(incident, ("row", "col"), shift_by))
    neighbour = jnp.stack(stacked, axis=1)
    near_inputs = jnp.take(neighbour, near_offsets[0] + 2, axis=1)
    local_near = near_tiles[0]
    real_prod = jnp.einsum(
        "wnpq,wnqc->wpc", local_near[:, :, 0], near_inputs, preferred_element_type=jnp.float32
    )
    imag_prod = jnp.einsum(
        "wnpq,wnqc->wpc", local_near[:, :, 1], near_inputs, preferred_element_type=jnp.float32
    )
    near_total = combine_parts(real_prod, imag_prod)
    rows_local = far_row[0, 0]
    cols_local = far_col[0, 0]
    rank_local = far_rank[0, 0]
    live_count = far_count[0, 0]
    group_limit = (live_count + 15) // 16
    outputs = []
    for wave_index in range(wave_count):
        wave_columns = lax.all_gather(incident[wave_index], "row", axis=0, tiled=True)
        wave_tiles = wave_columns.reshape(-1, tile_rows, columns)
        far_sum = far_partial(
            wave_tiles,
            rows_local,
            cols_local,
            rank_local,
            live_count,
            far_u[0, 0, wave_index],
            far_v[0, 0, wave_index],
            group_limit,
            row_blocks,
        )
        own_rows = reduce_rows(far_sum, row_blocks, tile_rows, columns)
        outputs.append(near_total[wave_index] + own_rows)
    return jnp.stack(outputs, axis=0).astype(jnp.bfloat16)


def solution(mesh):
    in_specs = (
        P(None, ("row", "col"), None),
        P(("row", "col"), None, None, None, None, None),
        P(("row", "col"), None),
        P("row", "col", None),
        P("row", "col", None),
        P("row", "col", None),
        P("row", "col"),
        P("row", "col", None, None, None, None, None),
        P("row", "col", None, None, None, None, None),
    )
    out_specs = P(None, ("row", "col"), None)
    return jax.shard_map(shards, mesh=mesh, in_specs=in_specs, out_specs=out_specs, check_vma=False)
```

profile of v0, /device:TPU:32, one launch (start us, length us, event | category | flops | bytes accessed | tf_op | source)
XLA Modules:
  0.0 776.4 jit_solution(10596356141134408394)
XLA Ops:
  9.9 2.8 fusion.68
  18.4 183.2 %all-gather.7.cloned.1.call-done = bf16[1,8192,512]{2,1,0:T(8,128)(2,1)} async-done(((bf16[1,256,512]{2,1,0:T(8,128)(2,1)}), bf16[1,8192,512]{2,1,0:T(8,128)(2,1)}) %all-gather.7.cloned.1.call-update) | async-done | bytes 8388624 | tf_op jit(solution)/shard_map/all_gather | solution.py:106
  201.6 2.5 broadcast.159.clone.1
  204.1 56.6 %while.23 = (s32[]{:T(128)}, f32[8,256,512]{2,1,0:T(8,128)}, s32[]{:T(128)}, s32[64]{0:T(128)S(1)}, bf16[64,2,32,256]{3,2,0,1:T(8,128)(2,1)S(1)}, /*index=5*/bf1...) while((s32[]{:T(128)}, f32[8,256,512]{2,1,0:T(8,128)}, ...), condition=%wide.region_6.8_spmd.clone, body=%wide.region_4.7_spmd.clone.sunk | while | flops 549194432 | bytes 109075392 | solution.py:72
  204.9 6.1 gather_fusion.1
  211.0 3.1 fusion.95
  214.1 3.2 fusion.94
  217.7 4.6 fusion.98
  222.3 4.6 fusion.97
  226.9 9.3 %slice_subtract_fusion.12 = (f32[16,256,256]{2,1,0:T(8,128)S(1)}, f32[16,256,256]{2,1,0:T(8,128)}) fusion(f32[16,256,512]{2,1,0:T(8,128)} %fusion.97, f32[16,256,512]{2,1,0:T(8,128)} %fusion.98), kind=kLoop, calls=%fused_computation.44.clone.1 | loop fusion | flops 2097152 | bytes 25165824 | tf_op jit(solution)/shard_map/while/body/sub | solution.py:17
  236.2 6.8 pad_maximum_fusion.7
  243.1 17.6 %scatter_fusion.1 = f32[8,256,512]{2,1,0:T(8,128)} fusion(f32[8,256,512]{2,1,0:T(8,128)} %get-tuple-element.465, s32[16]{0:T(128)S(1)} %compare_select_fusion.11, f32[16,256,512]{2,1,0:T(8,128)} %pad_maximum_fusion.7), kind=kCustom, calls=%fused_computation.4.clone.clone.1 | custom fusion | flops 2097152 | bytes 25165888 | tf_op jit(solution)/shard_map/while/body/scatter-add | solution.py:69
  260.7 5.4 copy.25
  266.2 127.1 %all-gather.5.cloned.1.call-done = bf16[1,8192,512]{2,1,0:T(8,128)(2,1)} async-done(((bf16[1,256,512]{2,1,0:T(8,128)(2,1)}), bf16[1,8192,512]{2,1,0:T(8,128)(2,1)}) %all-gather.5.cloned.1.call-update) | async-done | bytes 8388624 | tf_op jit(solution)/shard_map/all_gather | solution.py:106
  393.3 2.6 broadcast.159.clone
  395.9 58.2 %while.22 = (s32[]{:T(128)}, f32[8,256,512]{2,1,0:T(8,128)}, s32[]{:T(128)}, s32[64]{0:T(128)S(1)}, bf16[64,2,32,256]{3,2,0,1:T(8,128)(2,1)}, /*index=5*/bf16[64...) while((s32[]{:T(128)}, f32[8,256,512]{2,1,0:T(8,128)}, ...), condition=%wide.region_2.4_spmd.clone, body=%wide.region_0.3_spmd.clone.sunk | while | flops 549194432 | bytes 109063104 | solution.py:72
  396.6 6.2 gather_fusion
  402.8 3.1 fusion.88
  405.9 3.1 fusion.87
  409.5 5.6 fusion.91
  415.0 5.5 fusion.90
  420.5 9.2 %slice_subtract_fusion.10 = (f32[16,256,256]{2,1,0:T(8,128)S(1)}, f32[16,256,256]{2,1,0:T(8,128)}) fusion(f32[16,256,512]{2,1,0:T(8,128)} %fusion.90, f32[16,256,512]{2,1,0:T(8,128)} %fusion.91), kind=kLoop, calls=%fused_computation.11.clone.1 | loop fusion | flops 2097152 | bytes 25165824 | tf_op jit(solution)/shard_map/while/body/sub | solution.py:17
  429.7 6.7 pad_maximum_fusion.6
  436.5 17.7 %scatter_fusion = f32[8,256,512]{2,1,0:T(8,128)} fusion(f32[8,256,512]{2,1,0:T(8,128)} %get-tuple-element.420, s32[16]{0:T(128)S(1)} %compare_select_fusion.10, f32[16,256,512]{2,1,0:T(8,128)} %pad_maximum_fusion.6), kind=kCustom, calls=%fused_computation.3.clone.clone.1 | custom fusion | flops 2097152 | bytes 25165888 | tf_op jit(solution)/shard_map/while/body/scatter-add | solution.py:69
  454.2 5.4 copy.24
  460.6 223.4 %collective-permute-start = (bf16[2,256,512]{2,1,0:T(8,128)(2,1)S(1)}, bf16[2,256,512]{2,1,0:T(8,128)(2,1)S(1)}, u32[]{:S(2)}, u32[]{:S(2)}) collective-permute-start(bf16[2,256,512]{2,1,0:T(8,128)(2,1)S(1)} %copy-done.1), channel_id=1, source_target_pairs={{0,2},{1,3},{2,4},{3,5},{4,6},{5,7},{6,8},{7,9},{8,10},{9,11},{10,... | collective-permute-start | bytes 1572872 | tf_op jit(solution)/shard_map/ppermute | solution.py:10
  684.1 4.8 collective-permute-start.2
  690.3 31.0 %collective-permute-done = bf16[2,256,512]{2,1,0:T(8,128)(2,1)S(1)} collective-permute-done((bf16[2,256,512]{2,1,0:T(8,128)(2,1)S(1)}, bf16[2,256,512]{2,1,0:T(8,128)(2,1)S(1)}, u32[]{:S(2)}, u32[]{:S(2)}) %collective-permute-start) | collective-permute-done | bytes 524320 | tf_op jit(solution)/shard_map/ppermute | solution.py:10
  721.4 13.7 %collective-permute-done.2 = bf16[2,256,512]{2,1,0:T(8,128)(2,1)S(1)} collective-permute-done((bf16[2,256,512]{2,1,0:T(8,128)(2,1)S(1)}, bf16[2,256,512]{2,1,0:T(8,128)(2,1)S(1)}, u32[]{:S(2)}, u32[]{:S(2)}) %collective-permute-start.2) | collective-permute-done | bytes 524320 | tf_op jit(solution)/shard_map/ppermute | solution.py:10
  735.2 16.7 %collective-permute-done.3 = bf16[2,256,512]{2,1,0:T(8,128)(2,1)S(1)} collective-permute-done((bf16[2,256,512]{2,1,0:T(8,128)(2,1)S(1)}, bf16[2,256,512]{2,1,0:T(8,128)(2,1)S(1)}, u32[]{:S(2)}, u32[]{:S(2)}) %collective-permute-start.3) | collective-permute-done | bytes 524320 | tf_op jit(solution)/shard_map/ppermute | solution.py:10
  753.8 2.6 fusion.48
  758.5 9.0 %reduce-scatter.3.cloned.1.call-done = f32[256,512]{0,1:T(8,128)} async-done(((f32[2048,512]{0,1:T(8,128)}), f32[256,512]{0,1:T(8,128)}) %reduce-scatter.3.cloned.1.call-update) | async-done | bytes 524304 | tf_op jit(solution)/shard_map/reduce_scatter | solution.py:77
  (60 shorter events, 19.7 us)
Async XLA Ops:
  6.5 195.0 %all-gather.7.cloned.1.call-start = ((), (), s32[]{:S(2)}) async-start(), calls=%async_computation.5 | async-start | bytes 8650752 | tf_op jit(solution)/shard_map/all_gather | solution.py:106
  8.4 384.9 %all-gather.5.cloned.1.call-start = ((), (), s32[]{:S(2)}) async-start(), calls=%async_computation.4 | async-start | bytes 8650752 | tf_op jit(solution)/shard_map/all_gather | solution.py:106
  9.2 749.3 %reduce-scatter.5.cloned.1.call-start = ((), (), s32[]{:S(2)}) async-start(), calls=%async_computation.3 | async-start | bytes 4718592 | tf_op jit(solution)/shard_map/reduce_scatter | solution.py:77
  9.9 3.5 copy-start
  18.4 185.7 %copy-start.4 = (s32[1,1,64]{2,1,0:T(1,128)S(1)}, s32[1,1,64]{2,1,0:T(1,128)}, u32[]{:S(2)}) copy-start(s32[1,1,64]{2,1,0:T(1,128)} %param.19) | copy-start | bytes 772
  18.4 185.7 %copy-start.5 = (s32[1,1,64]{2,1,0:T(1,128)S(1)}, s32[1,1,64]{2,1,0:T(1,128)}, u32[]{:S(2)}) copy-start(s32[1,1,64]{2,1,0:T(1,128)} %param.18) | copy-start | bytes 772
  18.4 185.7 %copy-start.6 = (s32[1,1,64]{2,1,0:T(1,128)S(1)}, s32[1,1,64]{2,1,0:T(1,128)}, u32[]{:S(2)}) copy-start(s32[1,1,64]{2,1,0:T(1,128)} %param.20) | copy-start | bytes 772
  266.2 501.3 %reduce-scatter.3.cloned.1.call-start = ((), (), s32[]{:S(2)}) async-start(), calls=%async_computation.2 | async-start | bytes 4718592 | tf_op jit(solution)/shard_map/reduce_scatter | solution.py:77
  459.6 1.1 copy-start.1
  459.6 229.3 %copy-start.7 = (s32[1,3]{1,0:T(1,128)S(1)}, s32[1,3]{1,0:T(1,128)}, u32[]{:S(2)}) copy-start(s32[1,3]{1,0:T(1,128)} %param.17) | copy-start | bytes 40
  459.6 229.3 %copy-start.2 = (bf16[1,2,3,2,256,256]{5,4,3,2,1,0:T(8,128)(2,1)S(1)}, bf16[1,2,3,2,256,256]{5,4,3,2,1,0:T(8,128)(2,1)}, u32[]{:S(2)}) copy-start(bf16[1,2,3,2,256,256]{5,4,3,2,1,0:T(8,128)(2,1)} %param.16) | copy-start | bytes 4718596
  460.6 260.6 %collective-permute-start = (bf16[2,256,512]{2,1,0:T(8,128)(2,1)S(1)}, bf16[2,256,512]{2,1,0:T(8,128)(2,1)S(1)}, u32[]{:S(2)}, u32[]{:S(2)}) collective-permute-start(bf16[2,256,512]{2,1,0:T(8,128)(2,1)S(1)} %copy-done.1), channel_id=1, source_target_pairs={{0,2},{1,3},{2,4},{3,5},{4,6},{5,7},{6,8},{7,9},{8,10},{9,11},{10,... | collective-permute-start | bytes 1572872 | tf_op jit(solution)/shard_map/ppermute | solution.py:10
  684.1 37.2 %collective-permute-start.1 = (bf16[2,256,512]{2,1,0:T(8,128)(2,1)S(1)}, bf16[2,256,512]{2,1,0:T(8,128)(2,1)S(1)}, u32[]{:S(2)}, u32[]{:S(2)}) collective-permute-start(bf16[2,256,512]{2,1,0:T(8,128)(2,1)S(1)} %copy-done.1), channel_id=1, source_target_pairs={{0,1},{1,2},{2,3},{3,4},{4,5},{5,6},{6,7},{7,8},{8,9},{9,10},{10,1... | collective-permute-start | bytes 1572872 | tf_op jit(solution)/shard_map/ppermute | solution.py:10
  684.1 51.0 %collective-permute-start.2 = (bf16[2,256,512]{2,1,0:T(8,128)(2,1)S(1)}, bf16[2,256,512]{2,1,0:T(8,128)(2,1)S(1)}, u32[]{:S(2)}, u32[]{:S(2)}) collective-permute-start(bf16[2,256,512]{2,1,0:T(8,128)(2,1)S(1)} %copy-done.1), channel_id=1, source_target_pairs={{0,255},{1,0},{2,1},{3,2},{4,3},{5,4},{6,5},{7,6},{8,7},{9,8},{10,... | collective-permute-start | bytes 1572872 | tf_op jit(solution)/shard_map/ppermute | solution.py:10
  688.8 63.0 %collective-permute-start.3 = (bf16[2,256,512]{2,1,0:T(8,128)(2,1)S(1)}, bf16[2,256,512]{2,1,0:T(8,128)(2,1)S(1)}, u32[]{:S(2)}, u32[]{:S(2)}) collective-permute-start(bf16[2,256,512]{2,1,0:T(8,128)(2,1)S(1)} %copy-done.1), channel_id=1, source_target_pairs={{0,254},{1,255},{2,0},{3,1},{4,2},{5,3},{6,4},{7,5},{8,6},{9,7},{1... | collective-permute-start | bytes 1572872 | tf_op jit(solution)/shard_map/ppermute | solution.py:10
  753.8 2.6 copy-start.3
Sparse Core Ops, SparseCore 0:
  9.1 192.3 all-gather.6
  203.3 189.9 all-gather.4
  395.9 99.1 reduce-scatter.4
  497.5 269.9 reduce-scatter.2
where the time goes:
time: 779 us; the launch traced here: 776 us
  waiting for transfers between devices  381 us (49%)
  starting transfers between devices  228 us (29%)
  other arithmetic  71 us (9%)
  local copies, waits for them, and re-layouts  44.3 us (6%)
  matrix products  37.4 us (5%)
  between operations  13.9 us (2%)
    all_gather x2, waiting for transfers between devices, shards(): lax.all_gather(incident[wave_index], 'row', axis=0, tiled=True)  310 us
    ppermute x4, starting transfers between devices, from_behind(): return lax.ppermute(value, axis, pairs)  228 us
    ppermute x4, waiting for transfers between devices, from_behind(): return lax.ppermute(value, axis, pairs)  61.4 us
    scatter-add x2, other arithmetic, add_group(): return far_sum.at[rows_group].add(contrib)  35.3 us
    sub x5, other arithmetic, combine_parts(): real_prod[..., :half_width] - imag_prod[..., half_width:]  19.1 us
  transfers between devices with their start and end apart: 8, of which 6 were waited for; matrix products, arithmetic and copies ran while one was open for 19% of the time, Pallas kernels for 0%

commit v1 on v0

v1 whole, which is shorter than its diff:
```python
import functools

import jax
import jax.numpy as jnp
from jax import lax
from jax.experimental import pallas as pl
from jax.experimental.pallas import tpu as pltpu
from jax.sharding import PartitionSpec as P

MESH = pl.DeviceIdType.MESH
BF16 = jnp.bfloat16
F32 = jnp.float32

TILE, RANK, SLOTS, WAVES, HALF = 256, 32, 64, 2, 256
WIDTH = 2 * HALF
N_ROW, N_COL, NEAR = 32, 8, 3
PACK = 4
GROUPS = (SLOTS + N_COL * (PACK - 1)) // PACK
HOPS = 8
ROWS = ((0, 128), (0, 128), (128, 128), (128, 128))
LAST = ((0, 64), (64, 64), (128, 64), (192, 64))

T_COL, T_RANK = 0, SLOTS
T_USLOT = T_RANK + SLOTS
T_CSLOT = T_USLOT + PACK * GROUPS
T_SAME = T_CSLOT + PACK * GROUPS
T_LAST = T_SAME + GROUPS
T_NEAR = T_LAST + N_COL
T_SIZE = T_NEAR + NEAR


def scalar_table(far_row, far_col, far_rank, far_count, near_offsets):
    i32 = jnp.int32
    slot = jnp.arange(SLOTS, dtype=i32)
    block = jnp.arange(N_COL, dtype=i32)
    earlier = (slot[:, None] > slot[None, :]) & (far_row[:, None] == far_row[None, :])
    place = jnp.sum(earlier.astype(i32), axis=1)
    count = jnp.sum((far_row[:, None] == block[None, :]).astype(i32), axis=0)
    groups = (count + PACK - 1) // PACK
    below = jnp.where(far_row[:, None] > block[None, :], groups[None, :], 0)
    dest = PACK * jnp.sum(below, axis=1) + place
    end = jnp.sum(jnp.where(block[:, None] >= block[None, :], groups[None, :], 0), axis=1)
    spot = jnp.arange(PACK * GROUPS, dtype=i32)
    hit = dest[None, :] == spot[:, None]
    uslot = jnp.sum(jnp.where(hit, slot[None, :], 0), axis=1)
    cslot = SLOTS + jnp.sum(jnp.where(hit, slot[None, :] - SLOTS, 0), axis=1)
    group = jnp.arange(GROUPS, dtype=i32)
    opens = ((end - groups)[None, :] == group[:, None]) & (groups[None, :] > 0)
    same = 1 - jnp.sum(opens.astype(i32), axis=1)
    last = jnp.where(groups > 0, end, 0)
    rank = jnp.where(slot < far_count, far_rank, 0)
    return jnp.concatenate([far_col, rank, uslot, cslot, same, last, near_offsets + 2]).astype(i32)


def mod(value, size):
    return lax.rem(value + size, size)


def body(
    table, x_hbm, near_hbm, u_hbm, v_hbm, out_ref,
    tiles0, tiles1, coef, ugrp, u_buf, v_buf, near_buf, near_x, near_acc, part,
    half_out, half_in, far_out, far_in,
    load_sem, ring_send, ring_recv, pair_send, pair_recv, near_send, near_recv,
    half_send, half_recv, far_send, far_recv,
):
    tiles = (tiles0, tiles1)
    r, c = lax.axis_index("row"), lax.axis_index("col")
    zl, xy = lax.rem(r, 2), r // 2
    y, x = lax.rem(xy, 4), xy // 4
    core, zh = lax.rem(c, 2), c // 2
    spot = (4 * x + lax.rem(x + y, 4), 4 * y + lax.rem(x + y, 4))

    def chip_at(ring, position):
        p = mod(position, 16)
        lead = p // 4
        trail = mod(lax.rem(p, 4) - lead, 4)
        return 4 * lead + trail if ring == 0 else 4 * trail + lead

    streams = ((0, 1), (0, -1), (1, 1), (1, -1))
    ring_next = [(chip_at(ring, spot[ring] + way) * 2 + zl, c) for ring, way in streams]
    pair = (r + 1 - 2 * zl, c)
    twin = (r, c + 1 - 2 * core)
    flat = r * N_COL + c
    shifts = (-2, -1, 1, 2)

    def flat_id(value):
        value = mod(value, N_ROW * N_COL)
        return (value // N_COL, lax.rem(value, N_COL))

    near_to = [flat_id(flat + shift) for shift in shifts]
    far_to = [(r, mod(zh + step, 4) * 2 + core) for step in (1, 2, 3)]

    loads = []
    for w in range(WAVES):
        loads.append(pltpu.make_async_copy(x_hbm.at[w], tiles[w].at[r], load_sem.at[w]))
    loads.append(pltpu.make_async_copy(x_hbm, near_x.at[2], load_sem.at[2]))
    loads.append(pltpu.make_async_copy(near_hbm, near_buf, load_sem.at[3]))
    loads.append(pltpu.make_async_copy(u_hbm, u_buf, load_sem.at[4]))
    loads.append(pltpu.make_async_copy(v_hbm, v_buf, load_sem.at[5]))
    for load in loads:
        load.start()

    barrier = pltpu.get_barrier_semaphore()
    peers = ring_next + [pair, twin] + near_to + far_to
    for peer in peers:
        pl.semaphore_signal(barrier, inc=1, device_id=peer, device_id_type=MESH)
    pl.semaphore_wait(barrier, len(peers))

    def remote(src, dst, send, recv, to):
        return pltpu.make_async_remote_copy(
            src_ref=src, dst_ref=dst, send_sem=send, recv_sem=recv, device_id=to, device_id_type=MESH
        )

    def pair_copy(w, tile):
        return remote(tiles[w].at[tile], tiles[w].at[tile], pair_send.at[w], pair_recv.at[w], pair)

    def ring_copy(w, k, sub, s, tile, rows):
        piece = tiles[w].at[tile, pl.ds(*rows[s])]
        return remote(piece, piece, ring_send.at[w, k, sub, s], ring_recv.at[w, k, sub, s], ring_next[s])

    def origin(s, k, sub):
        ring, way = streams[s]
        plane = zl if sub == 0 else 1 - zl
        return chip_at(ring, spot[ring] - way * k) * 2 + plane

    def ring_start(w, sub):
        for s in range(4):
            ring_copy(w, 0, sub, s, origin(s, 0, sub), ROWS).start()

    def ring_forward(w, k, sub, rows):
        for s in range(4):
            tile = origin(s, k, sub)
            ring_copy(w, k - 1, sub, s, tile, ROWS).wait_recv()
            ring_copy(w, k, sub, s, tile, rows).start()

    def near_copy(i):
        return remote(x_hbm, near_x.at[(4, 3, 1, 0)[i]], near_send.at[i], near_recv.at[i], near_to[i])

    def group_u(w, g):
        stack = [u_buf[w, table[T_USLOT + PACK * g + i]] for i in range(PACK)]
        ugrp[w, g] = jnp.concatenate(stack, axis=0).T

    def near_product(w):
        def rows(b, carry):
            here = pl.ds(pl.multiple_of(b * 64, 64), 64)
            real = jnp.zeros((64, WIDTH), F32)
            imag = jnp.zeros((64, WIDTH), F32)
            for n in range(NEAR):
                at = near_x[table[T_NEAR + n], w]
                real += jnp.dot(near_buf[w, n, 0, here], at, preferred_element_type=F32)
                imag += jnp.dot(near_buf[w, n, 1, here], at, preferred_element_type=F32)
            near_acc[w, here, :HALF] = real[:, :HALF] - imag[:, HALF:]
            near_acc[w, here, HALF:] = real[:, HALF:] + imag[:, :HALF]
            return carry

        lax.fori_loop(0, TILE // 64, rows, 0)

    rank_row = lax.broadcasted_iota(jnp.int32, (RANK, HALF), 0)

    def coefficients(w, s):
        at = tiles[w][table[T_COL + s]]
        prod = jnp.dot(v_buf[w, s], at, preferred_element_type=F32)
        live = rank_row < table[T_RANK + s]
        real = jnp.where(live, prod[:RANK, :HALF] - prod[RANK:, HALF:], 0.0).astype(BF16)
        imag = jnp.where(live, prod[:RANK, HALF:] + prod[RANK:, :HALF], 0.0).astype(BF16)
        coef[s, :RANK, :HALF] = real
        coef[s, :RANK, HALF:] = imag
        coef[s, RANK:, :HALF] = -imag
        coef[s, RANK:, HALF:] = real

    def row_sums(w, g):
        same = table[T_SAME + g].astype(F32)
        stack = [coef[table[T_CSLOT + PACK * g + i]] for i in range(PACK)]
        right = jnp.concatenate(stack, axis=0)
        for b in range(2):
            here = pl.ds(b * 128, 128)
            prod = jnp.dot(ugrp[w, g, here], right, preferred_element_type=F32)
            part[g + 1, here] = prod + same * part[g, here]

    def half_copy(w):
        return remote(half_out.at[w], half_in.at[w], half_send.at[w], half_recv.at[w], twin)

    def far_copy(w, d):
        return remote(far_out.at[w, d], far_in.at[w, d], far_send.at[w, d], far_recv.at[w, d], far_to[d])

    def reduce_pack(w):
        for i in range(4):
            a = 2 * i + 1 - core
            half_out[w, i] = part[table[T_LAST + a]].astype(BF16)

    def reduce_send(w):
        half_copy(w).wait_recv()
        for d in range(3):
            to = mod(zh + d + 1, 4)
            both = part[table[T_LAST + 2 * to + core]] + half_in[w, to].astype(F32)
            far_out[w, d] = both.astype(BF16)
        near_acc[w] += part[table[T_LAST + 2 * zh + core]] + half_in[w, zh].astype(F32)

    def reduce_start(w):
        for d in (1, 0, 2):
            far_copy(w, d).start()

    def finish(w):
        total = near_acc[w]
        for d in range(3):
            far_copy(w, d).wait_recv()
            total += far_in[w, d].astype(F32)
        out_ref[w] = total.astype(BF16)

    def many(first, last, step, *head):
        def one(i, carry):
            step(*head, i)
            return carry

        lax.fori_loop(first, last, one, 0)

    work = {(w, k, sub): [] for w in range(WAVES) for k in range(HOPS) for sub in range(2)}

    def at(w, k, sub, fn, *args):
        work[w, k, sub].append(functools.partial(fn, *args))

    def clear():
        coef[SLOTS] = jnp.zeros((2 * RANK, WIDTH), BF16)
        part[0] = jnp.zeros((TILE, WIDTH), F32)

    at(0, 0, 1, clear)
    at(0, 1, 0, lambda: loads[4].wait())
    for step in range(11):
        at(0, 1 + step // 2, step % 2, many, 4 * step, 4 * step + 4, lambda j: group_u(j // GROUPS, lax.rem(j, GROUPS)))
    at(0, 6, 1, lambda: [load.wait() for load in (loads[2], loads[3], loads[5])])
    at(0, 6, 1, lambda: [near_copy(i).wait_recv() for i in range(4)])
    at(0, 6, 1, near_product, 0)
    at(0, 7, 0, near_product, 1)
    for step in range(8):
        at(1, step // 2, step % 2, many, 8 * step, 8 * step + 8, coefficients, 0)
    for step in range(4):
        low, high = GROUPS * step // 4, GROUPS * (step + 1) // 4
        at(1, 4 + step // 2, step % 2, many, low, high, row_sums, 0)
    at(1, 5, 1, reduce_pack, 0)
    at(1, 6, 0, lambda: half_copy(0).start())
    at(1, 6, 1, reduce_send, 0)
    at(1, 7, 0, lambda: reduce_start(0))

    loads[0].wait()
    pair_copy(0, r).start()
    ring_start(0, 0)
    loads[1].wait()
    pair_copy(1, r).start()
    for i in range(4):
        near_copy(i).start()

    def pump(w):
        for k in range(HOPS):
            for sub in range(2):
                if k == 0 and sub == 0:
                    pass
                elif k == 0:
                    pair_copy(w, r + 1 - 2 * zl).wait_recv()
                    ring_start(w, 1)
                else:
                    ring_forward(w, k, sub, LAST if k == HOPS - 1 else ROWS)
                for item in work[w, k, sub]:
                    item()

    def drain(w):
        for sub in range(2):
            for s in range(4):
                ring_copy(w, HOPS - 1, sub, s, origin(s, HOPS, sub), LAST).wait_recv()

    pump(0)
    ring_start(1, 0)
    drain(0)
    pump(1)
    drain(1)

    many(0, SLOTS, coefficients, 1)
    many(0, GROUPS, row_sums, 1)
    reduce_pack(1)
    half_copy(1).start()
    finish(0)
    reduce_send(1)
    reduce_start(1)
    finish(1)

    for w in range(WAVES):
        pair_copy(w, r).wait_send()
        half_copy(w).wait_send()
        for d in range(3):
            far_copy(w, d).wait_send()
        for k in range(HOPS):
            for sub in range(2):
                for s in range(4):
                    ring_copy(w, k, sub, s, r, LAST if k == HOPS - 1 else ROWS).wait_send()
    for i in range(4):
        near_copy(i).wait_send()


def shards(incident, near_tiles, near_offsets, far_row, far_col, far_rank, far_count, far_u, far_v):
    table = scalar_table(far_row[0, 0], far_col[0, 0], far_rank[0, 0], far_count[0, 0], near_offsets[0])
    anywhere = pl.BlockSpec(memory_space=pl.ANY)
    dma = pltpu.SemaphoreType.DMA
    return pl.pallas_call(
        body,
        out_shape=jax.ShapeDtypeStruct((WAVES, TILE, WIDTH), BF16),
        in_specs=[pl.BlockSpec(memory_space=pltpu.SMEM)] + [anywhere] * 4,
        out_specs=pl.BlockSpec(memory_space=pltpu.VMEM),
        scratch_shapes=[
            pltpu.VMEM((N_ROW, TILE, WIDTH), BF16),
            pltpu.VMEM((N_ROW, TILE, WIDTH), BF16),
            pltpu.VMEM((SLOTS + 1, 2 * RANK, WIDTH), BF16),
            pltpu.VMEM((WAVES, GROUPS, TILE, PACK * 2 * RANK), BF16),
            pltpu.VMEM((WAVES, SLOTS, 2 * RANK, TILE), BF16),
            pltpu.VMEM((WAVES, SLOTS, 2 * RANK, TILE), BF16),
            pltpu.VMEM((WAVES, NEAR, 2, TILE, TILE), BF16),
            pltpu.VMEM((5, WAVES, TILE, WIDTH), BF16),
            pltpu.VMEM((WAVES, TILE, WIDTH), F32),
            pltpu.VMEM((GROUPS + 1, TILE, WIDTH), F32),
            pltpu.VMEM((WAVES, 4, TILE, WIDTH), BF16),
            pltpu.VMEM((WAVES, 4, TILE, WIDTH), BF16),
            pltpu.VMEM((WAVES, 3, TILE, WIDTH), BF16),
            pltpu.VMEM((WAVES, 3, TILE, WIDTH), BF16),
            dma((6,)),
            dma((WAVES, HOPS, 2, 4)),
            dma((WAVES, HOPS, 2, 4)),
            dma((WAVES,)),
            dma((WAVES,)),
            dma((4,)),
            dma((4,)),
            dma((WAVES,)),
            dma((WAVES,)),
            dma((WAVES, 3)),
            dma((WAVES, 3)),
        ],
        compiler_params=pltpu.CompilerParams(
            collective_id=0, has_side_effects=True, vmem_limit_bytes=67_043_328
        ),
    )(
        table,
        incident,
        near_tiles[0],
        far_u[0, 0].reshape(WAVES, SLOTS, 2 * RANK, TILE),
        far_v[0, 0].reshape(WAVES, SLOTS, 2 * RANK, TILE),
    )


def solution(mesh):
    in_specs = (
        P(None, ("row", "col"), None),
        P(("row", "col"), None, None, None, None, None),
        P(("row", "col"), None),
        P("row", "col", None),
        P("row", "col", None),
        P("row", "col", None),
        P("row", "col"),
        P("row", "col", None, None, None, None, None),
        P("row", "col", None, None, None, None, None),
    )
    out_specs = P(None, ("row", "col"), None)
    return jax.shard_map(shards, mesh=mesh, in_specs=in_specs, out_specs=out_specs, check_vma=False)
```

time: 779 us -> 177 us (0.23)
  the two profiles are of different devices: /device:TPU:32 before, /device:TPU:1 now
where the time goes in v1:
time: 177 us
  Pallas kernels  169 us (95%)
  other arithmetic  4.07 us (2%)
  local copies, waits for them, and re-layouts  3.19 us (2%)
    pallas_call x1, Pallas kernels, shards(): pl.pallas_call(body, out_shape=jax.ShapeDtypeStruct((WAVES, TILE, WIDTH),...  169 us

profile of v1, /device:TPU:1, one launch (start us, length us, event | category | flops | bytes accessed | tf_op | source)
XLA Modules:
  0.0 177.1 jit_solution(7724604765067649196)
XLA Ops:
  0.7 0.7 compare_select_fusion
  1.3 0.7 add_bitcast_fusion
  2.0 0.8 convert_reduce_fusion.2
  2.7 0.9 convert_reduce_fusion
  3.7 0.1 select_reduce_fusion.2
  3.8 0.7 select_reduce_fusion.3
  4.5 0.1 convert_reduce_fusion.1
  4.6 0.1 select_reduce_fusion
  4.7 1.3 concatenate.3.table
  6.1 169.2 %shard_map.91 = bf16[2,256,512]{2,1,0:T(8,128)(2,1)} custom-call(s32[337]{0:T(512)} %concatenate.3.table, bf16[2,256,512]{2,1,0:T(8,128)(2,1)} %x_hbm.1, bf16[2,3,2,256,256]{4,3,2,1,0:T(8,128)(2,1)} %bitcast.13, bf16[2,64,64,256]{3,2,1,0:T(8,128)(2,1)} %bitcast.11, bf16[2,64,64,256]{3,2,1,0:T(8,128)(2,1)} %bitcast.12), custom_call_target="tpu_custom_call" | custom-call | tf_op jit(solution)/shard_map/pallas_call | solution.py:302
  175.3 1.9 %copy.12 = bf16[2,256,512]{2,1,0:T(8,128)(2,1)} copy(bf16[2,256,512]{2,1,0:T(8,128)(2,1)} %shard_map.91) | data formatting | bytes 1048576
  (5 shorter events, 0.0 us)

commit v2 on v0

v2 whole, which is shorter than its diff:
```python
import functools

import jax
import jax.numpy as jnp
from jax import lax
from jax.experimental import pallas as pl
from jax.experimental.pallas import tpu as pltpu
from jax.sharding import PartitionSpec as P

MESH = pl.DeviceIdType.MESH
BF16 = jnp.bfloat16
F32 = jnp.float32

TILE, RANK, SLOTS, WAVES, HALF = 256, 32, 64, 2, 256
WIDTH = 2 * HALF
N_ROW, N_COL, NEAR = 32, 8, 3
PACK = 4
GROUPS = (SLOTS + N_COL * (PACK - 1)) // PACK
HOPS = 8
ROWS = ((0, 128), (0, 128), (128, 128), (128, 128))
LAST = ((0, 64), (64, 64), (128, 64), (192, 64))

CHUNKS = 2 * WAVES
LANES = 128
PART = 2 * LANES
EAGER = 0.9
STARTS = (0.0, 0.0, 0.0, 52.0)
WIRE, HOP = 1.4, 2.6


def gather_order():
    paired = {q: max(2.8 * (q + 1), STARTS[q] - 5.2) + HOP for q in range(CHUNKS)}
    ready = {(q, sub): max(STARTS[q], paired[q] * sub) for q in range(CHUNKS) for sub in range(2)}
    hop = dict.fromkeys(ready, 0)
    now = free = 0.0
    when = []
    while hop:
        soon = max(now, free - WIRE, min(ready[x] for x in hop))
        q, sub = pick = min((x for x in hop if ready[x] <= soon + 1e-9), key=lambda x: (x[0], ready[x], x))
        when.append((soon, (q, hop[pick], sub)))
        now = max(now, ready[pick]) + 0.1
        free = max(now, free) + (WIRE if hop[pick] < HOPS - 1 else WIRE / 2)
        ready[pick] = free + HOP
        hop[pick] += 1
        if hop[pick] == HOPS:
            del hop[pick]
            if not any(x[0] == q for x in hop):
                when.append((free + HOP, ("drain", q)))
    when.sort(key=lambda x: x[0])
    return [(step, nxt - time) for (time, step), (nxt, _) in zip(when, when[1:] + when[-1:])]


def mod(value, size):
    return lax.rem(value + size, size)


def body(
    row_hbm, col_hbm, rank_hbm, count_hbm, offset_hbm, x_hbm, near_hbm, u_hbm, v_hbm, out_ref,
    tiles0, tiles1, tiles2, tiles3, near_x0, near_x1, near_x2, near_x3,
    coef, ugrp, u_buf, v_buf, near_buf, near_acc, part,
    half_out, half_in, far_out, far_in, held,
    row_buf, plan_buf, plan, far_col, far_rank, far_count, near_offset,
    small_sem, plan_sem, x_sem, load_sem, ring_send, ring_recv, pair_send, pair_recv, near_send, near_recv,
    half_send, half_recv, far_send, far_recv,
):
    tiles = (tiles0, tiles1, tiles2, tiles3)
    near_x = (near_x0, near_x1, near_x2, near_x3)
    r, c = lax.axis_index("row"), lax.axis_index("col")
    zl, xy = lax.rem(r, 2), r // 2
    y, x = lax.rem(xy, 4), xy // 4
    core, zh = lax.rem(c, 2), c // 2
    spot = (4 * x + lax.rem(x + y, 4), 4 * y + lax.rem(x + y, 4))

    def chip_at(ring, position):
        p = mod(position, 16)
        lead = p // 4
        trail = mod(lax.rem(p, 4) - lead, 4)
        return 4 * lead + trail if ring == 0 else 4 * trail + lead

    streams = ((0, 1), (0, -1), (1, 1), (1, -1))
    ring_next = [(chip_at(ring, spot[ring] + way) * 2 + zl, c) for ring, way in streams]
    pair_row = r + 1 - 2 * zl
    pair = (pair_row, c)
    twin = (r, c + 1 - 2 * core)
    far_up, far_down = ((r, mod(zh + step, 4) * 2 + core) for step in (1, -1))

    line = 4 * zl + zh

    def on_line(place):
        place = mod(place, 8)
        return (2 * xy + place // 4, 2 * lax.rem(place, 4) + core)

    near_to = (on_line(line + 1), on_line(line - 1), twin, twin)
    up_wraps, down_wraps = line == 7, line == 0
    up_row = mod(r - 2 * (line // 7), N_ROW)
    down_row = mod(r + 2 * (1 - (line + 6) // 7), N_ROW)

    small = [
        pltpu.make_async_copy(src, dst, small_sem.at[i])
        for i, (src, dst) in enumerate((
            (row_hbm, row_buf), (col_hbm, far_col), (rank_hbm, far_rank), (count_hbm, far_count), (offset_hbm, near_offset),
        ))
    ]
    x_loads = []
    for q in range(CHUNKS):
        for i in range(2):
            src = x_hbm.at[q // 2, :, pl.ds(HALF * i + LANES * (q % 2), LANES)]
            for n, dst in enumerate((tiles[q].at[r], near_x[q].at[2])):
                x_loads.append(pltpu.make_async_copy(src, dst.at[:, pl.ds(LANES * i, LANES)], x_sem.at[q, n]))
    loads = [
        pltpu.make_async_copy(src, dst, load_sem.at[i])
        for i, (src, dst) in enumerate(((near_hbm, near_buf), (u_hbm, u_buf), (v_hbm, v_buf)))
    ]
    for load in x_loads + small + loads:
        load.start()

    barrier = pltpu.get_barrier_semaphore()
    peers = ring_next + [pair, twin] + list(near_to[:2]) + [far_up, far_down]
    for peer in peers:
        pl.semaphore_signal(barrier, inc=1, device_id=peer, device_id_type=MESH)
    pl.semaphore_wait(barrier, len(peers))

    def remote(src, dst, send, recv, to):
        return pltpu.make_async_remote_copy(
            src_ref=src, dst_ref=dst, send_sem=send, recv_sem=recv, device_id=to, device_id_type=MESH
        )

    def pair_copy(q, tile):
        return remote(tiles[q].at[tile], tiles[q].at[tile], pair_send.at[q], pair_recv.at[q], pair)

    def ring_copy(q, k, sub, s, tile, rows):
        piece = tiles[q].at[tile, pl.ds(*rows[s])]
        return remote(piece, piece, ring_send.at[q], ring_recv.at[q, k, sub], ring_next[s])

    def origin(s, k, sub):
        ring, way = streams[s]
        plane = zl if sub == 0 else 1 - zl
        return chip_at(ring, spot[ring] - way * k) * 2 + plane

    def ring_wait(q, k, sub):
        both = tiles[q].at[pl.ds(0, 1 if k == HOPS - 1 else 2)]
        remote(both, both, ring_send.at[q], ring_recv.at[q, k, sub], ring_next[0]).wait_recv()

    def forward(q, k, sub):
        rows = LAST if k == HOPS - 1 else ROWS
        if k > 0:
            ring_wait(q, k - 1, sub)
        elif sub == 1:
            pair_copy(q, pair_row).wait_recv()
        for s in range(4):
            ring_copy(q, k, sub, s, origin(s, k, sub), rows).start()

    def ring_sent(q):
        everything = tiles[q].at[pl.ds(0, 30)]
        remote(everything, everything, ring_send.at[q], ring_recv.at[q, 0, 0], ring_next[0]).wait_send()

    def drain(q):
        for sub in range(2):
            ring_wait(q, HOPS - 1, sub)

    def near_copy(q, i):
        src = (
            tiles[q].at[up_row], tiles[q].at[down_row], tiles[q].at[r], near_x[q].at[4 - 4 * core],
        )[i]
        dst = near_x[q].at[(0, 4, 1 + 2 * core, 3 - 2 * core)[i]]
        return remote(src, dst, near_send.at[q], near_recv.at[q, i], near_to[i])

    def near_early(q):
        near_copy(q, 2).start()

        @pl.when(jnp.logical_not(up_wraps))
        def _():
            near_copy(q, 0).start()

        @pl.when(jnp.logical_not(down_wraps))
        def _():
            near_copy(q, 1).start()

    def near_late(q):
        @pl.when(up_wraps)
        def _():
            near_copy(q, 0).start()

        @pl.when(down_wraps)
        def _():
            near_copy(q, 1).start()

    def near_relay(q):
        near_copy(q, 0).wait_recv()
        near_copy(q, 1).wait_recv()
        near_copy(q, 3).start()

    def near_arrived(q):
        near_copy(q, 2).wait_recv()
        near_copy(q, 3).wait_recv()

    def make_plan():
        small[0].wait()

        def number(shape, dim):
            return lax.broadcasted_iota(jnp.int32, shape, dim)

        def total(mask, value, axis):
            return jnp.sum(jnp.where(mask, value, 0), axis=axis, keepdims=True, dtype=jnp.int32)

        square, wide, low = (SLOTS, SLOTS), (SLOTS, 128), (N_COL, 128)
        rows_on_lanes = jnp.broadcast_to(row_buf[...], square)
        i, j = number(square, 0), number(square, 1)
        rows = total(i == j, rows_on_lanes, 1)
        place = total((rows_on_lanes == rows) & (j < i), 1, 1)
        a = number(wide, 1)
        count = total(a == rows, 1, 0)
        groups = lax.shift_right_logical(count + (PACK - 1), 2)
        dest = PACK * total(a < rows, jnp.broadcast_to(groups, wide), 1) + place
        slot = number(wide, 0)
        uslot = total(dest == a, slot, 0)
        cslot = SLOTS + total(dest == a, slot - SLOTS, 0)
        b, lane = number(low, 0), number(low, 1)
        groups_low = jnp.broadcast_to(groups, low)
        own = total(b == lane, groups_low, 1)
        end = total(lane <= b, groups_low, 1)
        same = 1 - total((end - own == lane) & (own > 0), 1, 0)
        last = total(b == lane, jnp.where(own > 0, end, 0), 0)
        plan_buf[...] = jnp.concatenate([uslot, cslot, same, last] * 2, axis=0)
        copy = pltpu.make_async_copy(plan_buf, plan, plan_sem)
        copy.start()
        coef[SLOTS] = jnp.zeros((2 * RANK, PART), BF16)
        part[0] = jnp.zeros((TILE, PART), F32)
        copy.wait()

    def within(index, most):
        return jnp.minimum(jnp.maximum(index, 0), most)

    def group_u(w, g):
        stack = [u_buf[w, within(plan[0, PACK * g + i], SLOTS - 1)] for i in range(PACK)]
        ugrp[w, g] = jnp.concatenate(stack, axis=0).T

    def near_product(q):
        w = q // 2

        def rows(b, carry):
            here = pl.ds(pl.multiple_of(b * 128, 128), 128)
            real = jnp.zeros((128, PART), F32)
            imag = jnp.zeros((128, PART), F32)
            for n in range(NEAR):
                at = near_x[q][near_offset[0, n] + 2]
                real += jnp.dot(near_buf[w, n, 0, here], at, preferred_element_type=F32)
                imag += jnp.dot(near_buf[w, n, 1, here], at, preferred_element_type=F32)
            near_acc[q, here, :LANES] = real[:, :LANES] - imag[:, LANES:]
            near_acc[q, here, LANES:] = real[:, LANES:] + imag[:, :LANES]
            return carry

        lax.fori_loop(0, TILE // 128, rows, 0)

    rank_row = lax.broadcasted_iota(jnp.int32, (RANK, LANES), 0)

    def coefficients(q, s):
        at = tiles[q][far_col[0, s]]
        prod = jnp.dot(v_buf[q // 2, s], at, preferred_element_type=F32)
        live = rank_row < jnp.where(s < far_count[0, 0], far_rank[0, s], 0)
        real = jnp.where(live, prod[:RANK, :LANES] - prod[RANK:, LANES:], 0.0).astype(BF16)
        imag = jnp.where(live, prod[:RANK, LANES:] + prod[RANK:, :LANES], 0.0).astype(BF16)
        coef[s, :RANK, :LANES] = real
        coef[s, :RANK, LANES:] = imag
        coef[s, RANK:, :LANES] = -imag
        coef[s, RANK:, LANES:] = real

    def row_sums(q, g):
        same = plan[2, g].astype(F32)
        stack = [coef[within(plan[1, PACK * g + i], SLOTS)] for i in range(PACK)]
        right = jnp.concatenate(stack, axis=0)
        prod = jnp.dot(ugrp[q // 2, g], right, preferred_element_type=F32)
        part[g + 1] = prod + same * part[g]

    def row_part(a):
        return part[within(plan[3, a], GROUPS)]

    def half_copy(q, i):
        return remote(half_out.at[q, i], half_in.at[q, i], half_send.at[q], half_recv.at[q, i], twin)

    upper, lower = pl.ds(0, 128), pl.ds(128, 128)
    moves = ((1, upper, far_up), (1, lower, far_down), (0, lower, far_up), (2, upper, far_down), (0, upper, far_up), (2, lower, far_down))

    def far_copy(q, m):
        d, rows, to = moves[m]
        return remote(far_out.at[q, d, rows], far_in.at[q, d, rows], far_send.at[q], far_recv.at[q, m], to)

    turns = [mod(zh + step, 4) for step in (2, 1, 3, 0)]

    def reduce_pack(q):
        for n, i in enumerate(turns):
            half_out[q, i] = row_part(2 * i + 1 - core).astype(BF16)
            if n:
                half_copy(q, turns[n - 1]).start()
        half_copy(q, turns[3]).start()

    def reduce_pass(q):
        for n, i in enumerate(turns):
            half_copy(q, i).wait_recv()
            both = row_part(2 * i + core) + half_in[q, i].astype(F32)
            if n == 0:
                far_out[q, 1] = both.astype(BF16)
            elif n == 1:
                far_out[q, 0, lower] = both[128:].astype(BF16)
                held[0] = both[:128]
                far_copy(q, 0).start()
                far_copy(q, 1).start()
            elif n == 2:
                far_out[q, 2, upper] = both[:128].astype(BF16)
                held[1] = both[128:]
                far_copy(q, 2).start()
            else:
                near_acc[q] += both
                far_copy(q, 3).start()

    def reduce_relay(q):
        far_copy(q, 0).wait_recv()
        far_out[q, 0, upper] = (held[0] + far_in[q, 1, upper].astype(F32)).astype(BF16)
        far_copy(q, 1).wait_recv()
        far_out[q, 2, lower] = (held[1] + far_in[q, 1, lower].astype(F32)).astype(BF16)
        far_copy(q, 4).start()
        far_copy(q, 5).start()

    def finish(q):
        for m in (2, 3, 4, 5):
            far_copy(q, m).wait_recv()
        total = near_acc[q] + far_in[q, 0].astype(F32) + far_in[q, 2].astype(F32)
        here = LANES * (q % 2)
        out_ref[q // 2, :, here : here + LANES] = total[:, :LANES].astype(BF16)
        out_ref[q // 2, :, HALF + here : HALF + here + LANES] = total[:, LANES:].astype(BF16)

    def many(first, last, step, *head, unroll=1):
        def one(i, carry):
            for n in range(unroll):
                step(*head, i * unroll + n)
            return carry

        lax.fori_loop(first // unroll, last // unroll, one, 0)

    def tag(name, cost, fn, *args, **kw):
        def run():
            with jax.named_scope(name):
                fn(*args, **kw)

        return cost, run

    def far_work(q):
        yield from (tag(f"V{q}", 0.42, many, 8 * i, 8 * i + 8, coefficients, q, unroll=4) for i in range(SLOTS // 8))
        if q:
            yield tag(f"rel{q - 1}", 0.3, reduce_relay, q - 1)
        yield tag(f"nrel{q}", 0.1, near_relay, q)
        yield tag(f"U{q}", 0.7, many, 0, 6, row_sums, q, unroll=2)
        yield tag(f"U{q}", 0.7, many, 6, 12, row_sums, q, unroll=2)
        yield tag(f"U{q}", 0.7, many, 12, 18, row_sums, q, unroll=2)
        yield tag(f"U{q}", 0.5, many, 18, GROUPS, row_sums, q, unroll=2)
        yield tag(f"pack{q}", 0.3, reduce_pack, q)
        yield tag(f"near{q}", 0.6, near_all, q)
        yield tag(f"pass{q}", 0.7, reduce_pass, q)

    def near_all(q):
        near_arrived(q)
        near_product(q)

    def pair_start(q):
        pair_copy(q, r).start()

    def near_own():
        for q in range(CHUNKS):
            pltpu.make_async_copy(near_x[q].at[2], near_x[q].at[2], x_sem.at[q, 1]).wait()

    def early():
        yield tag("plan", 1.2, make_plan)
        yield tag("lu", 0.1, lambda: loads[1].wait())
        for i in range(11):
            yield tag("ugrp", 0.4, many, 4 * i, 4 * i + 4, lambda n: group_u(n // GROUPS, lax.rem(n, GROUPS)))
        yield tag("ld", 0.1, lambda: [load.wait() for load in small[1:] + [loads[0], loads[2]]])
        yield tag("ldx", 0.1, near_own)

    def load_chunk(q):
        pltpu.make_async_copy(tiles[q].at[r], tiles[q].at[r], x_sem.at[q, 0]).wait()

    load_chunk(0)
    pair_copy(0, r).start()
    forward(0, 0, 0)
    load_chunk(1)
    pair_copy(1, r).start()
    forward(1, 0, 0)
    load_chunk(2)
    load_chunk(3)
    queue = list(early())
    later = [
        (9, near_early, 0), (13, pair_start, 2), (18, near_early, 1), (24, pair_start, 3), (28, near_early, 2), (36, near_early, 3),
    ]
    time = 0.0
    credit = 0.0
    for step, gap in gather_order():
        if step[0] == "drain":
            with jax.named_scope(f"drain{step[1]}"):
                drain(step[1])
            if step[1] < CHUNKS - 1:
                queue += far_work(step[1])
        elif step not in ((0, 0, 0), (1, 0, 0)):
            with jax.named_scope("F%d%d%d" % step):
                forward(*step)
            if step[1:] == (6, 1):
                near_late(step[0])
        time += gap
        while later and later[0][0] <= time:
            _, send, q = later.pop(0)
            send(q)
        credit = min(credit + EAGER * gap, 3.0)
        while queue and credit >= queue[0][0] * 0.6:
            credit -= queue[0][0]
            queue.pop(0)[1]()
    for _, run in queue + list(far_work(CHUNKS - 1)):
        run()
    with jax.named_scope("rel3"):
        reduce_relay(CHUNKS - 1)
    with jax.named_scope("sent"):
        for q in range(CHUNKS):
            ring_sent(q)
            pair_copy(q, r).wait_send()
            remote(half_out.at[q], half_in.at[q], half_send.at[q], half_recv.at[q, 0], twin).wait_send()
            four = near_x[q].at[pl.ds(0, 4)]
            remote(four, four, near_send.at[q], near_recv.at[q, 0], twin).wait_send()
    for q in range(CHUNKS):
        with jax.named_scope(f"fin{q}"):
            finish(q)
            remote(far_out.at[q], far_in.at[q], far_send.at[q], far_recv.at[q, 0], far_up).wait_send()


def shards(incident, near_tiles, near_offsets, far_row, far_col, far_rank, far_count, far_u, far_v):
    dma = pltpu.SemaphoreType.DMA
    return pl.pallas_call(
        body,
        out_shape=jax.ShapeDtypeStruct((WAVES, TILE, WIDTH), BF16),
        in_specs=[pl.BlockSpec(memory_space=pl.ANY)] * 9,
        out_specs=pl.BlockSpec(memory_space=pltpu.VMEM),
        scratch_shapes=[pltpu.VMEM((N_ROW, TILE, PART), BF16)] * CHUNKS
        + [pltpu.VMEM((5, TILE, PART), BF16)] * CHUNKS
        + [
            pltpu.VMEM((SLOTS + 1, 2 * RANK, PART), BF16),
            pltpu.VMEM((WAVES, GROUPS, TILE, PACK * 2 * RANK), BF16),
            pltpu.VMEM((WAVES, SLOTS, 2 * RANK, TILE), BF16),
            pltpu.VMEM((WAVES, SLOTS, 2 * RANK, TILE), BF16),
            pltpu.VMEM((WAVES, NEAR, 2, TILE, TILE), BF16),
            pltpu.VMEM((CHUNKS, TILE, PART), F32),
            pltpu.VMEM((GROUPS + 1, TILE, PART), F32),
            pltpu.VMEM((CHUNKS, 4, TILE, PART), BF16),
            pltpu.VMEM((CHUNKS, 4, TILE, PART), BF16),
            pltpu.VMEM((CHUNKS, 3, TILE, PART), BF16),
            pltpu.VMEM((CHUNKS, 3, TILE, PART), BF16),
            pltpu.VMEM((2, 128, PART), F32),
            pltpu.VMEM((1, SLOTS), jnp.int32),
            pltpu.VMEM((8, 128), jnp.int32),
            pltpu.SMEM((8, 128), jnp.int32),
            pltpu.SMEM((1, SLOTS), jnp.int32),
            pltpu.SMEM((1, SLOTS), jnp.int32),
            pltpu.SMEM((1, 1), jnp.int32),
            pltpu.SMEM((1, NEAR), jnp.int32),
            dma((5,)),
            dma,
            dma((CHUNKS, 2)),
            dma((3,)),
            dma((CHUNKS,)),
            dma((CHUNKS, HOPS, 2)),
            dma((CHUNKS,)),
            dma((CHUNKS,)),
            dma((CHUNKS,)),
            dma((CHUNKS, 4)),
            dma((CHUNKS,)),
            dma((CHUNKS, 4)),
            dma((CHUNKS,)),
            dma((CHUNKS, 6)),
        ],
        compiler_params=pltpu.CompilerParams(
            collective_id=0, has_side_effects=True, vmem_limit_bytes=67_043_328
        ),
    )(
        far_row[0],
        far_col[0],
        far_rank[0],
        far_count,
        near_offsets,
        incident,
        near_tiles[0],
        far_u[0, 0].reshape(WAVES, SLOTS, 2 * RANK, TILE),
        far_v[0, 0].reshape(WAVES, SLOTS, 2 * RANK, TILE),
    )


def solution(mesh):
    in_specs = (
        P(None, ("row", "col"), None),
        P(("row", "col"), None, None, None, None, None),
        P(("row", "col"), None),
        P("row", "col", None),
        P("row", "col", None),
        P("row", "col", None),
        P("row", "col"),
        P("row", "col", None, None, None, None, None),
        P("row", "col", None, None, None, None, None),
    )
    out_specs = P(None, ("row", "col"), None)
    return jax.shard_map(shards, mesh=mesh, in_specs=in_specs, out_specs=out_specs, check_vma=False)
```

time: 779 us -> 129 us (0.17)
  the two profiles are of different devices: /device:TPU:32 before, /device:TPU:1 now
where the time goes in v2:
time: 129 us
  Pallas kernels  127 us (98%)
  local copies, waits for them, and re-layouts  1.87 us (1%)
    pallas_call x1, Pallas kernels, shards(): pl.pallas_call(body, out_shape=jax.ShapeDtypeStruct((WAVES, TILE, WIDTH),...  127 us

profile of v2, /device:TPU:1, one launch (start us, length us, event | category | flops | bytes accessed | tf_op | source)
XLA Modules:
  0.0 129.1 jit_solution(9769495951465381959)
XLA Ops:
  0.7 126.6 %shard_map.91 = bf16[2,256,512]{2,1,0:T(8,128)(2,1)} custom-call(s32[1,64]{1,0:T(1,128)} %bitcast.9, s32[1,64]{1,0:T(1,128)} %bitcast.10, s32[1,64]{1,0:T(1,128)} %bitcast.11, s32[1,1]{1,0:T(1,128)S(6)} %copy.11.count_hbm, s32[1,3]{1,0:T(1,128)} %offset_hbm.1, bf16[2,256,512]{2,1,0:T(8,128)(2,1)} %x_hbm.1, bf16[2,3,2,256,256]{4,3,2,1,0:T(8,128)(2,1)} %bitcast.8, ...), custom_call_target="tpu_custom_call" | custom-call | tf_op jit(solution)/shard_map/pallas_call | solution.py:434
  127.3 1.9 %copy.12 = bf16[2,256,512]{2,1,0:T(8,128)(2,1)} copy(bf16[2,256,512]{2,1,0:T(8,128)(2,1)} %shard_map.91) | data formatting | bytes 1048576

commit v3 on v2

--- a/solution.py
+++ b/solution.py
@@ -23,31 +23,87 @@
 CHUNKS = 2 * WAVES
 LANES = 128
 PART = 2 * LANES
-EAGER = 0.9
-STARTS = (0.0, 0.0, 0.0, 52.0)
+STARTS = (0.0, 0.0, 0.0, 44.0)
 WIRE, HOP = 1.4, 2.6
 
 
-def gather_order():
+SHORT = {0: 6, 1: 6}
+CROSS_TIME = 10.0
+QUEUE = 1.5
+TWIN_TIME, RELAY_TIME, FAR_TIME, NEAR_TIME = 1.7, 7.0, 7.0, 2.5
+BUSY = 6.0
+V_PIECES, U_PIECES, G_PIECES = 8, 2, 11
+V_UNROLL, U_UNROLL = 8, 11
+U_COST = 2.2
+
+
+def hops_of(q, sub):
+    return SHORT.get(q, HOPS) if sub == 1 else HOPS
+
+
+def work_items():
+    items = {("plan",): (0, 0.9, {}), ("u_loaded",): (1, 0.1, {("plan",): 2.0})}
+    for i in range(G_PIECES):
+        items["group", i] = (2, 0.39, {("u_loaded",): 0.0})
+    items["loaded",] = (3, 0.1, {("group", G_PIECES - 1): 0.0})
+    for time, name in ((9, ("near_early", 0)), (13, ("pair", 2)), (18, ("near_early", 1)), (24, ("pair", 3)), (28, ("near_early", 2)), (36, ("near_early", 3))):
+        items[name] = (-1, 0.05, {("start",): time})
+    for q in range(CHUNKS):
+        for i in range(V_PIECES):
+            items["V", q, i] = (10 * q + 10, 2.5 / V_PIECES, {("drain", q): 0.0, ("loaded",): 0.0, ("U", q - 1, U_PIECES - 1): 0.0})
+        for i in range(U_PIECES):
+            items["U", q, i] = (10 * q + 11, U_COST / U_PIECES, {("V", q, V_PIECES - 1): 0.0, ("pass", q - 2): 0.0})
+        items["pack", q] = (10 * q + 12, 0.3, {("U", q, U_PIECES - 1): 0.0})
+        items["pass", q] = (10 * q + 13, 0.6, {("pack", q): TWIN_TIME, ("relay", q - 2): 0.0})
+        items["relay", q] = (10 * q + 14, 0.25, {("pass", q): RELAY_TIME + BUSY * (q < 2)})
+        items["near_relay", q] = (10 * q + 15, 0.1, {("drain", q): 1.0})
+        items["near", q] = (100 + q, 0.55, {("near_relay", q): NEAR_TIME, ("loaded",): 0.0})
+        items["finish", q] = (110 + q, 0.3, {("relay", q): FAR_TIME, ("near", q): 0.0, ("drain", CHUNKS - 1): 0.0})
+    return items
+
+
+def schedule():
     paired = {q: max(2.8 * (q + 1), STARTS[q] - 5.2) + HOP for q in range(CHUNKS)}
     ready = {(q, sub): max(STARTS[q], paired[q] * sub) for q in range(CHUNKS) for sub in range(2)}
     hop = dict.fromkeys(ready, 0)
+    here = {}
+    items = work_items()
+    ended = {("start",): 0.0}
     now = free = 0.0
-    when = []
-    while hop:
-        soon = max(now, free - WIRE, min(ready[x] for x in hop))
-        q, sub = pick = min((x for x in hop if ready[x] <= soon + 1e-9), key=lambda x: (x[0], ready[x], x))
-        when.append((soon, (q, hop[pick], sub)))
-        now = max(now, ready[pick]) + 0.1
-        free = max(now, free) + (WIRE if hop[pick] < HOPS - 1 else WIRE / 2)
-        ready[pick] = free + HOP
-        hop[pick] += 1
-        if hop[pick] == HOPS:
-            del hop[pick]
-            if not any(x[0] == q for x in hop):
-                when.append((free + HOP, ("drain", q)))
-    when.sort(key=lambda x: x[0])
-    return [(step, nxt - time) for (time, step), (nxt, _) in zip(when, when[1:] + when[-1:])]
+    order = []
+    while hop or items:
+        ripe = [x for x in hop if ready[x] <= now + 1e-9]
+        if ripe and free - now <= QUEUE:
+            q, sub = pick = min(ripe, key=lambda x: (x[0], ready[x], x))
+            order.append(("step", q, hop[pick], sub))
+            now += 0.12
+            free = max(now, free) + (WIRE if hop[pick] < HOPS - 1 else WIRE / 2)
+            ready[pick] = free + HOP
+            hop[pick] += 1
+            if hop[pick] == hops_of(q, sub):
+                del hop[pick]
+                here[pick] = ready[pick]
+                if sub == 0 and q in SHORT:
+                    items["cross", q] = (-2, 0.1, {("start",): ready[pick]})
+                    here[pick] += CROSS_TIME
+                if (q, 0) in here and (q, 1) in here:
+                    items["drain", q] = (-2, 0.05, {("start",): max(here[q, 0], here[q, 1])})
+            continue
+        open_at = {}
+        for name, (rank, cost, after) in items.items():
+            known = {k: v for k, v in after.items() if k[-1] != -1 and k[1:2] != (-1,) and k[1:2] != (-2,)}
+            if all(k in ended for k in known):
+                open_at[name] = max([0.0] + [ended[k] + v for k, v in known.items()])
+        can = [x for x in open_at if open_at[x] <= now + 1e-9]
+        if can:
+            name = min(can, key=lambda x: (items[x][0], [n for n in x[1:]]))
+            order.append(name)
+            now += items.pop(name)[1]
+            ended[name] = now
+            continue
+        soon = [open_at[x] for x in open_at] + [max(ready[x], free - QUEUE) for x in hop]
+        now = max(now + 1e-6, min(soon))
+    return order
 
 
 def mod(value, size):
@@ -55,13 +111,13 @@
 
 
 def body(
-    row_hbm, col_hbm, rank_hbm, count_hbm, offset_hbm, x_hbm, near_hbm, u_hbm, v_hbm, out_ref,
+    row_hbm, col_hbm, rank_hbm, count_hbm, offset_hbm, x_hbm, near_hbm, u_hbm, v_hbm, out_hbm,
     tiles0, tiles1, tiles2, tiles3, near_x0, near_x1, near_x2, near_x3,
     coef, ugrp, u_buf, v_buf, near_buf, near_acc, part,
-    half_out, half_in, far_out, far_in, held,
+    half_out, half_in, far_out, far_in, held, own_acc, out_buf,
     row_buf, plan_buf, plan, far_col, far_rank, far_count, near_offset,
     small_sem, plan_sem, x_sem, load_sem, ring_send, ring_recv, pair_send, pair_recv, near_send, near_recv,
-    half_send, half_recv, far_send, far_recv,
+    half_send, half_recv, far_send, far_recv, cross_send, cross_recv, out_sem,
 ):
     tiles = (tiles0, tiles1, tiles2, tiles3)
     near_x = (near_x0, near_x1, near_x2, near_x3)
@@ -151,19 +207,38 @@
             ring_copy(q, k, sub, s, origin(s, k, sub), rows).start()
 
     def ring_sent(q):
-        everything = tiles[q].at[pl.ds(0, 30)]
+        everything = tiles[q].at[pl.ds(0, 15 + 2 * SHORT[q] if q in SHORT else 30)]
         remote(everything, everything, ring_send.at[q], ring_recv.at[q, 0, 0], ring_next[0]).wait_send()
 
+    def cross_start(q, k):
+        for s in range(4 if k < HOPS else 1):
+            piece = tiles[q].at[origin(s, k, 0)]
+            piece = piece.at[pl.ds(*ROWS[s])] if k < HOPS else piece
+            remote(piece, piece, cross_send.at[q], cross_recv.at[q, HOPS - k], pair).start()
+
+    def cross_wait(q):
+        for k in range(SHORT[q] + 1, HOPS + 1):
+            got = tiles[q].at[pl.ds(0, 2 if k < HOPS else 1)]
+            remote(got, got, cross_send.at[q], cross_recv.at[q, HOPS - k], pair).wait_recv()
+
+    def cross(q):
+        ring_wait(q, HOPS - 1, 0)
+        cross_start(q, HOPS)
+
     def drain(q):
-        for sub in range(2):
-            ring_wait(q, HOPS - 1, sub)
+        if q in SHORT:
+            ring_wait(q, SHORT[q] - 1, 1)
+            cross_wait(q)
+        else:
+            ring_wait(q, HOPS - 1, 0)
+            ring_wait(q, HOPS - 1, 1)
 
     def near_copy(q, i):
         src = (
             tiles[q].at[up_row], tiles[q].at[down_row], tiles[q].at[r], near_x[q].at[4 - 4 * core],
         )[i]
         dst = near_x[q].at[(0, 4, 1 + 2 * core, 3 - 2 * core)[i]]
-        return remote(src, dst, near_send.at[q], near_recv.at[q, i], near_to[i])
+        return remote(src, dst, near_send.at[q], near_recv.at[q, i // 2], near_to[i])
 
     def near_early(q):
         near_copy(q, 2).start()
@@ -186,13 +261,12 @@
             near_copy(q, 1).start()
 
     def near_relay(q):
-        near_copy(q, 0).wait_recv()
-        near_copy(q, 1).wait_recv()
+        near_wait(q, 0)
         near_copy(q, 3).start()
 
-    def near_arrived(q):
-        near_copy(q, 2).wait_recv()
-        near_copy(q, 3).wait_recv()
+    def near_wait(q, part):
+        two = near_x[q].at[pl.ds(0, 2)]
+        remote(two, two, near_send.at[q], near_recv.at[q, part], twin).wait_recv()
 
     def make_plan():
         small[0].wait()
@@ -225,7 +299,8 @@
         copy = pltpu.make_async_copy(plan_buf, plan, plan_sem)
         copy.start()
         coef[SLOTS] = jnp.zeros((2 * RANK, PART), BF16)
-        part[0] = jnp.zeros((TILE, PART), F32)
+        for n in range(2):
+            part[n, 0] = jnp.zeros((TILE, PART), F32)
         copy.wait()
 
     def within(index, most):
@@ -266,14 +341,15 @@
         coef[s, RANK:, LANES:] = real
 
     def row_sums(q, g):
+        sums = part.at[q % 2]
         same = plan[2, g].astype(F32)
         stack = [coef[within(plan[1, PACK * g + i], SLOTS)] for i in range(PACK)]
         right = jnp.concatenate(stack, axis=0)
         prod = jnp.dot(ugrp[q // 2, g], right, preferred_element_type=F32)
-        part[g + 1] = prod + same * part[g]
-
-    def row_part(a):
-        return part[within(plan[3, a], GROUPS)]
+        sums[g + 1] = prod + same * sums[g]
+
+    def row_part(q, a):
+        return part[q % 2, within(plan[3, a], GROUPS)]
 
     def half_copy(q, i):
         return remote(half_out.at[q, i], half_in.at[q, i], half_send.at[q], half_recv.at[q, i], twin)
@@ -283,13 +359,13 @@
 
     def far_copy(q, m):
         d, rows, to = moves[m]
-        return remote(far_out.at[q, d, rows], far_in.at[q, d, rows], far_send.at[q], far_recv.at[q, m], to)
+        return remote(far_out.at[q, d, rows], far_in.at[q, d, rows], far_send.at[q], far_recv.at[q, min(m // 2, 1)], to)
 
     turns = [mod(zh + step, 4) for step in (2, 1, 3, 0)]
 
     def reduce_pack(q):
         for n, i in enumerate(turns):
-            half_out[q, i] = row_part(2 * i + 1 - core).astype(BF16)
+            half_out[q, i] = row_part(q, 2 * i + 1 - core).astype(BF16)
             if n:
                 half_copy(q, turns[n - 1]).start()
         half_copy(q, turns[3]).start()
@@ -297,37 +373,47 @@
     def reduce_pass(q):
         for n, i in enumerate(turns):
             half_copy(q, i).wait_recv()
-            both = row_part(2 * i + core) + half_in[q, i].astype(F32)
+            both = row_part(q, 2 * i + core) + half_in[q, i].astype(F32)
             if n == 0:
                 far_out[q, 1] = both.astype(BF16)
             elif n == 1:
                 far_out[q, 0, lower] = both[128:].astype(BF16)
-                held[0] = both[:128]
+                held[q % 2, 0] = both[:128]
                 far_copy(q, 0).start()
                 far_copy(q, 1).start()
             elif n == 2:
                 far_out[q, 2, upper] = both[:128].astype(BF16)
-                held[1] = both[128:]
+                held[q % 2, 1] = both[128:]
                 far_copy(q, 2).start()
             else:
-                near_acc[q] += both
+                own_acc[q] = both
                 far_copy(q, 3).start()
 
     def reduce_relay(q):
-        far_copy(q, 0).wait_recv()
-        far_out[q, 0, upper] = (held[0] + far_in[q, 1, upper].astype(F32)).astype(BF16)
-        far_copy(q, 1).wait_recv()
-        far_out[q, 2, lower] = (held[1] + far_in[q, 1, lower].astype(F32)).astype(BF16)
+        got = far_in.at[q, 1]
+        remote(got, got, far_send.at[q], far_recv.at[q, 0], far_up).wait_recv()
+        far_out[q, 0, upper] = (held[q % 2, 0] + far_in[q, 1, upper].astype(F32)).astype(BF16)
+        far_out[q, 2, lower] = (held[q % 2, 1] + far_in[q, 1, lower].astype(F32)).astype(BF16)
         far_copy(q, 4).start()
         far_copy(q, 5).start()
 
     def finish(q):
-        for m in (2, 3, 4, 5):
-            far_copy(q, m).wait_recv()
-        total = near_acc[q] + far_in[q, 0].astype(F32) + far_in[q, 2].astype(F32)
-        here = LANES * (q % 2)
-        out_ref[q // 2, :, here : here + LANES] = total[:, :LANES].astype(BF16)
-        out_ref[q // 2, :, HALF + here : HALF + here + LANES] = total[:, LANES:].astype(BF16)
+        got = far_in.at[q, pl.ds(0, 2)]
+        remote(got, got, far_send.at[q], far_recv.at[q, 1], far_up).wait_recv()
+        total = near_acc[q] + own_acc[q] + far_in[q, 0].astype(F32) + far_in[q, 2].astype(F32)
+        out_buf[q] = total.astype(BF16)
+        for copy in out_copies(q):
+            copy.start()
+
+    def out_copies(q):
+        return [
+            pltpu.make_async_copy(
+                out_buf.at[q, :, pl.ds(LANES * i, LANES)],
+                out_hbm.at[q // 2, :, pl.ds(HALF * i + LANES * (q % 2), LANES)],
+                out_sem.at[q],
+            )
+            for i in range(2)
+        ]
 
     def many(first, last, step, *head, unroll=1):
         def one(i, carry):
@@ -337,28 +423,8 @@
 
         lax.fori_loop(first // unroll, last // unroll, one, 0)
 
-    def tag(name, cost, fn, *args, **kw):
-        def run():
-            with jax.named_scope(name):
-                fn(*args, **kw)
-
-        return cost, run
-
-    def far_work(q):
-        yield from (tag(f"V{q}", 0.42, many, 8 * i, 8 * i + 8, coefficients, q, unroll=4) for i in range(SLOTS // 8))
-        if q:
-            yield tag(f"rel{q - 1}", 0.3, reduce_relay, q - 1)
-        yield tag(f"nrel{q}", 0.1, near_relay, q)
-        yield tag(f"U{q}", 0.7, many, 0, 6, row_sums, q, unroll=2)
-        yield tag(f"U{q}", 0.7, many, 6, 12, row_sums, q, unroll=2)
-        yield tag(f"U{q}", 0.7, many, 12, 18, row_sums, q, unroll=2)
-        yield tag(f"U{q}", 0.5, many, 18, GROUPS, row_sums, q, unroll=2)
-        yield tag(f"pack{q}", 0.3, reduce_pack, q)
-        yield tag(f"near{q}", 0.6, near_all, q)
-        yield tag(f"pass{q}", 0.7, reduce_pass, q)
-
     def near_all(q):
-        near_arrived(q)
+        near_wait(q, 1)
         near_product(q)
 
     def pair_start(q):
@@ -368,13 +434,16 @@
         for q in range(CHUNKS):
             pltpu.make_async_copy(near_x[q].at[2], near_x[q].at[2], x_sem.at[q, 1]).wait()
 
-    def early():
-        yield tag("plan", 1.2, make_plan)
-        yield tag("lu", 0.1, lambda: loads[1].wait())
-        for i in range(11):
-            yield tag("ugrp", 0.4, many, 4 * i, 4 * i + 4, lambda n: group_u(n // GROUPS, lax.rem(n, GROUPS)))
-        yield tag("ld", 0.1, lambda: [load.wait() for load in small[1:] + [loads[0], loads[2]]])
-        yield tag("ldx", 0.1, near_own)
+    def all_sent():
+        for q in range(CHUNKS):
+            ring_sent(q)
+            pair_copy(q, r).wait_send()
+            remote(half_out.at[q], half_in.at[q], half_send.at[q], half_recv.at[q, 0], twin).wait_send()
+            four = near_x[q].at[pl.ds(0, 4)]
+            remote(four, four, near_send.at[q], near_recv.at[q, 0], twin).wait_send()
+            if q in SHORT:
+                crossed = tiles[q].at[pl.ds(0, 1 + 2 * (HOPS - 1 - SHORT[q]))]
+                remote(crossed, crossed, cross_send.at[q], cross_recv.at[q, 0], pair).wait_send()
 
     def load_chunk(q):
         pltpu.make_async_copy(tiles[q].at[r], tiles[q].at[r], x_sem.at[q, 0]).wait()
@@ -387,46 +456,44 @@
     forward(1, 0, 0)
     load_chunk(2)
     load_chunk(3)
-    queue = list(early())
-    later = [
-        (9, near_early, 0), (13, pair_start, 2), (18, near_early, 1), (24, pair_start, 3), (28, near_early, 2), (36, near_early, 3),
-    ]
-    time = 0.0
-    credit = 0.0
-    for step, gap in gather_order():
-        if step[0] == "drain":
-            with jax.named_scope(f"drain{step[1]}"):
-                drain(step[1])
-            if step[1] < CHUNKS - 1:
-                queue += far_work(step[1])
-        elif step not in ((0, 0, 0), (1, 0, 0)):
-            with jax.named_scope("F%d%d%d" % step):
-                forward(*step)
-            if step[1:] == (6, 1):
-                near_late(step[0])
-        time += gap
-        while later and later[0][0] <= time:
-            _, send, q = later.pop(0)
-            send(q)
-        credit = min(credit + EAGER * gap, 3.0)
-        while queue and credit >= queue[0][0] * 0.6:
-            credit -= queue[0][0]
-            queue.pop(0)[1]()
-    for _, run in queue + list(far_work(CHUNKS - 1)):
-        run()
-    with jax.named_scope("rel3"):
-        reduce_relay(CHUNKS - 1)
-    with jax.named_scope("sent"):
-        for q in range(CHUNKS):
-            ring_sent(q)
-            pair_copy(q, r).wait_send()
-            remote(half_out.at[q], half_in.at[q], half_send.at[q], half_recv.at[q, 0], twin).wait_send()
-            four = near_x[q].at[pl.ds(0, 4)]
-            remote(four, four, near_send.at[q], near_recv.at[q, 0], twin).wait_send()
+    def step(q, k, sub):
+        if (q, k, sub) not in ((0, 0, 0), (1, 0, 0)):
+            forward(q, k, sub)
+        if (k, sub) == (6, 0):
+            near_late(q)
+        if (k, sub) == (7, 0) and SHORT.get(q) == 6:
+            cross_start(q, 7)
+
+    def group_piece(i):
+        each = WAVES * GROUPS // G_PIECES
+        many(each * i, each * i + each, lambda n: group_u(n // GROUPS, lax.rem(n, GROUPS)))
+
+    def v_piece(q, i):
+        each = SLOTS // V_PIECES
+        many(each * i, each * i + each, coefficients, q, unroll=V_UNROLL)
+
+    def u_piece(q, i):
+        cuts = [GROUPS * n // U_PIECES for n in range(U_PIECES + 1)]
+        many(cuts[i], cuts[i + 1], row_sums, q, unroll=U_UNROLL)
+
+    def loaded():
+        for load in small[1:] + [loads[0], loads[2]]:
+            load.wait()
+        near_own()
+
+    run = {
+        "step": step, "cross": cross, "drain": drain, "plan": make_plan, "u_loaded": loads[1].wait, "group": group_piece,
+        "loaded": loaded, "near_early": near_early, "pair": pair_start, "V": v_piece, "U": u_piece, "pack": reduce_pack,
+        "pass": reduce_pass, "relay": reduce_relay, "near_relay": near_relay, "near": near_all, "finish": finish,
+    }
+    for name in schedule():
+        if name == ("finish", CHUNKS - 1):
+            all_sent()
+        with jax.named_scope("_".join(str(x) for x in name)):
+            run[name[0]](*name[1:])
     for q in range(CHUNKS):
-        with jax.named_scope(f"fin{q}"):
-            finish(q)
-            remote(far_out.at[q], far_in.at[q], far_send.at[q], far_recv.at[q, 0], far_up).wait_send()
+        remote(far_out.at[q], far_in.at[q], far_send.at[q], far_recv.at[q, 0], far_up).wait_send()
+        pltpu.make_async_copy(out_buf.at[q], out_buf.at[q], out_sem.at[q]).wait()
 
 
 def shards(incident, near_tiles, near_offsets, far_row, far_col, far_rank, far_count, far_u, far_v):
@@ -435,7 +502,7 @@
         body,
         out_shape=jax.ShapeDtypeStruct((WAVES, TILE, WIDTH), BF16),
         in_specs=[pl.BlockSpec(memory_space=pl.ANY)] * 9,
-        out_specs=pl.BlockSpec(memory_space=pltpu.VMEM),
+        out_specs=pl.BlockSpec(memory_space=pl.ANY),
         scratch_shapes=[pltpu.VMEM((N_ROW, TILE, PART), BF16)] * CHUNKS
         + [pltpu.VMEM((5, TILE, PART), BF16)] * CHUNKS
         + [
@@ -445,12 +512,14 @@
             pltpu.VMEM((WAVES, SLOTS, 2 * RANK, TILE), BF16),
             pltpu.VMEM((WAVES, NEAR, 2, TILE, TILE), BF16),
             pltpu.VMEM((CHUNKS, TILE, PART), F32),
-            pltpu.VMEM((GROUPS + 1, TILE, PART), F32),
+            pltpu.VMEM((2, GROUPS + 1, TILE, PART), F32),
             pltpu.VMEM((CHUNKS, 4, TILE, PART), BF16),
             pltpu.VMEM((CHUNKS, 4, TILE, PART), BF16),
             pltpu.VMEM((CHUNKS, 3, TILE, PART), BF16),
             pltpu.VMEM((CHUNKS, 3, TILE, PART), BF16),
-            pltpu.VMEM((2, 128, PART), F32),
+            pltpu.VMEM((2, 2, 128, PART), F32),
+            pltpu.VMEM((CHUNKS, TILE, PART), F32),
+            pltpu.VMEM((CHUNKS, TILE, PART), BF16),
             pltpu.VMEM((1, SLOTS), jnp.int32),
             pltpu.VMEM((8, 128), jnp.int32),
             pltpu.SMEM((8, 128), jnp.int32),
@@ -467,11 +536,14 @@
             dma((CHUNKS,)),
             dma((CHUNKS,)),
             dma((CHUNKS,)),
+            dma((CHUNKS, 2)),
+            dma((CHUNKS,)),
             dma((CHUNKS, 4)),
             dma((CHUNKS,)),
-            dma((CHUNKS, 4)),
-            dma((CHUNKS,)),
-            dma((CHUNKS, 6)),
+            dma((CHUNKS, 2)),
+            dma((CHUNKS,)),
+            dma((CHUNKS, 2)),
+            dma((CHUNKS,)),
         ],
         compiler_params=pltpu.CompilerParams(
             collective_id=0, has_side_effects=True, vmem_limit_bytes=67_043_328

time: 129 us -> 117 us (0.907)
  Pallas kernels: 127 us -> 115 us
    pallas_call x1, Pallas kernels: 127 us -> 115 us  [shards(): pl.pallas_call(body, out_shape=jax.ShapeDtypeStruct((WAVES, TILE, WIDTH),...]
where the time goes in v3:
time: 117 us
  Pallas kernels  115 us (98%)
  local copies, waits for them, and re-layouts  1.87 us (2%)
    pallas_call x1, Pallas kernels, shards(): pl.pallas_call(body, out_shape=jax.ShapeDtypeStruct((WAVES, TILE, WIDTH),...  115 us

profile of v3, /device:TPU:1, one launch (start us, length us, event | category | flops | bytes accessed | tf_op | source)
XLA Modules:
  0.0 117.2 jit_solution(16906064300829439537)
XLA Ops:
  0.7 114.7 %shard_map.91 = bf16[2,256,512]{2,1,0:T(8,128)(2,1)} custom-call(s32[1,64]{1,0:T(1,128)} %bitcast.9, s32[1,64]{1,0:T(1,128)} %bitcast.10, s32[1,64]{1,0:T(1,128)} %bitcast.11, s32[1,1]{1,0:T(1,128)S(6)} %copy.11.count_hbm, s32[1,3]{1,0:T(1,128)} %offset_hbm.1, bf16[2,256,512]{2,1,0:T(8,128)(2,1)} %x_hbm.1, bf16[2,3,2,256,256]{4,3,2,1,0:T(8,128)(2,1)} %bitcast.8, ...), custom_call_target="tpu_custom_call" | custom-call | tf_op jit(solution)/shard_map/pallas_call | solution.py:501
  115.4 1.9 %copy.12 = bf16[2,256,512]{2,1,0:T(8,128)(2,1)} copy(bf16[2,256,512]{2,1,0:T(8,128)(2,1)} %shard_map.91) | data formatting | bytes 1048576
